TPU v7x, 512 devices: a whole 4x8x8 slice. The times are simulated.
512 devices in a mesh: dp: 16 (over z, core), expert: 8 (over y), sequence: 4 (over x).
Axes of the slice: x: 4, y: 8, z: 8, core: 2. Of those that a mesh axis runs over, the one named last changes fastest.
Arguments:
- tokens: bfloat16 [1536, 3072], P(('dp', 'sequence')), may hold values from -6 to 6
- cotangent: bfloat16 [1536, 3072], P(('dp', 'sequence')), may hold values from -4 to 4
- experts: int32 [1536, 2], P(('dp', 'sequence')), may hold values from 0 to 7, all different within a row; in each aligned block of 24 rows (0 to 23, 24 to 47, ...) at most 10 rows name the same one
- gate_weights: float32 [1536, 2], P(('dp', 'sequence')), may hold values from 0.1 to 1
- w_gate: bfloat16 [8, 8192, 3072], P('expert', ('dp', 'sequence')), may hold values from -0.109375 to 0.109375
- w_up: bfloat16 [8, 8192, 3072], P('expert', ('dp', 'sequence')), may hold values from -0.109375 to 0.109375
- w_down: bfloat16 [8, 8192, 3072], P('expert', ('dp', 'sequence')), may hold values from -0.0625 to 0.0625
Outputs:
- output: bfloat16 [1536, 3072], P(('dp', 'sequence'), 'expert')
- grad_tokens: bfloat16 [1536, 3072], P(('dp', 'sequence'), 'expert')
- grad_w_gate: bfloat16 [8, 8192, 3072], P('expert', ('dp', 'sequence'))
- grad_w_up: bfloat16 [8, 8192, 3072], P('expert', ('dp', 'sequence'))
- grad_w_down: bfloat16 [8, 8192, 3072], P('expert', ('dp', 'sequence'))
Inputs may be any that keep to these rules, and one draw needn't show every extreme that they name: `experts`: A token's two ids differ. Within the rows of one device (aligned blocks of 24 rows) no id is named by more than 10 rows, a bound that some block reaches.
All inputs are finite; a program needn't handle non-finite values.
Results may differ from a plain program's by a relative error of at most 0.019.
Values may be sent and summed in bfloat16 or wider, within the bound.
No kernel may reach another device: no remote copies, remote signals or barrier semaphores. Data moves between devices by JAX's collectives and lax.ppermute only.
A program may use at most 128 MiB of HBM per device.

v0:
```python
import jax
import jax.numpy as jnp
from jax import lax
from jax.sharding import PartitionSpec as P

C = 10
HIGH = lax.Precision.HIGHEST


def on_device(tokens, cotangent, experts, gate_weights, w_gate, w_up, w_down):
    local = w_gate.shape[0]
    model_width = tokens.shape[1]
    first_id = lax.axis_index("expert") * local
    local_ids = first_id + jnp.arange(local, dtype=jnp.int32)
    chosen = (experts[:, :, None] == local_ids[None, None, :]).astype(jnp.int32)
    routed = jnp.sum(chosen, axis=1)
    gate_of = jnp.sum(gate_weights[:, :, None] * chosen.astype(jnp.float32), axis=1)
    slot_of = jnp.cumsum(routed, axis=0) - routed
    slot_ids = jnp.arange(C, dtype=jnp.int32)
    placing = (
        (slot_of.T[:, None, :] == slot_ids[None, :, None]) & (routed.T[:, None, :] == 1)
    ).astype(jnp.float32)
    placing_half = placing.astype(jnp.bfloat16)
    slot_gate = jnp.einsum("ect,te->ec", placing, gate_of, precision=HIGH)
    slot_tokens = jnp.einsum(
        "ect,td->ecd", placing_half, tokens, preferred_element_type=jnp.float32
    ).astype(jnp.bfloat16)
    picked_grad = jnp.einsum(
        "ect,td->ecd", placing_half, cotangent, preferred_element_type=jnp.float32
    )
    scaled_grad = (picked_grad * slot_gate[:, :, None]).astype(jnp.bfloat16)
    dp_count = lax.axis_size("dp")
    seq_count = lax.axis_size("sequence")
    seq_index = lax.axis_index("sequence")
    every_tok, every_grad = (
        lax.all_gather(slot_tokens, ("dp", "sequence"), axis=1, tiled=True),
        lax.all_gather(scaled_grad, ("dp", "sequence"), axis=1, tiled=True),
    )
    grid_tok = every_tok.reshape(local, dp_count, seq_count, C, model_width)
    grid_grad = every_grad.reshape(local, dp_count, seq_count, C, model_width)
    own_tok = lax.dynamic_index_in_dim(grid_tok, seq_index, 2, keepdims=False).reshape(
        local, dp_count * C, model_width
    )
    own_grad = lax.dynamic_index_in_dim(grid_grad, seq_index, 2, keepdims=False).reshape(
        local, dp_count * C, model_width
    )
    gate_rows, up_rows, down_rows = (
        lax.all_gather(w_gate, "sequence", axis=1, tiled=True),
        lax.all_gather(w_up, "sequence", axis=1, tiled=True),
        lax.all_gather(w_down, "sequence", axis=1, tiled=True),
    )
    pre_gate = jnp.einsum("erd,ehd->erh", own_tok, gate_rows, preferred_element_type=jnp.float32)
    pre_up = jnp.einsum("erd,ehd->erh", own_tok, up_rows, preferred_element_type=jnp.float32)
    sigmoid_gate = jax.nn.sigmoid(pre_gate)
    activated = pre_gate * sigmoid_gate
    hidden = (activated * pre_up).astype(jnp.bfloat16)
    out_part = jnp.einsum("erh,ehd->erd", hidden, down_rows, preferred_element_type=jnp.float32)
    out_part = lax.optimization_barrier(out_part.astype(jnp.bfloat16)).astype(jnp.float32)
    grad_hidden = jnp.einsum(
        "erd,ehd->erh", own_grad, down_rows, preferred_element_type=jnp.float32
    )
    grad_gate = (
        grad_hidden * pre_up * sigmoid_gate * (1.0 + pre_gate * (1.0 - sigmoid_gate))
    ).astype(jnp.bfloat16)
    grad_up = (grad_hidden * activated).astype(jnp.bfloat16)
    din_part = jnp.einsum("erh,ehd->erd", grad_gate, gate_rows, preferred_element_type=jnp.float32)
    din_part = din_part + jnp.einsum(
        "erh,ehd->erd", grad_up, up_rows, preferred_element_type=jnp.float32
    )
    din_part = lax.optimization_barrier(din_part.astype(jnp.bfloat16)).astype(jnp.float32)
    gate_cols, up_cols, hidden_cols = (
        lax.all_to_all(grad_gate, "sequence", split_axis=2, concat_axis=1, tiled=True),
        lax.all_to_all(grad_up, "sequence", split_axis=2, concat_axis=1, tiled=True),
        lax.all_to_all(hidden, "sequence", split_axis=2, concat_axis=1, tiled=True),
    )
    block_units = gate_cols.shape[2]
    gate_grid = gate_cols.reshape(local, seq_count, dp_count, C, block_units)
    up_grid = up_cols.reshape(local, seq_count, dp_count, C, block_units)
    hidden_grid = hidden_cols.reshape(local, seq_count, dp_count, C, block_units)
    form = "espch,epscd->ehd"
    grad_w_gate = jnp.einsum(form, gate_grid, grid_tok, preferred_element_type=jnp.float32).astype(
        jnp.bfloat16
    )
    grad_w_up = jnp.einsum(form, up_grid, grid_tok, preferred_element_type=jnp.float32).astype(
        jnp.bfloat16
    )
    grad_w_down = jnp.einsum(
        form, hidden_grid, grid_grad, preferred_element_type=jnp.float32
    ).astype(jnp.bfloat16)
    expert_out, expert_din = (
        lax.psum_scatter(
            out_part.astype(jnp.bfloat16), "dp", scatter_dimension=1, tiled=True
        ).astype(jnp.float32),
        lax.psum_scatter(
            din_part.astype(jnp.bfloat16), "dp", scatter_dimension=1, tiled=True
        ).astype(jnp.float32),
    )
    out_term = jnp.einsum(
        "ect,ecd->td", placing * slot_gate[:, :, None], expert_out, precision=HIGH
    )
    din_term = jnp.einsum("ect,ecd->td", placing, expert_din, precision=HIGH)
    out_total, din_total = (
        lax.psum_scatter(
            out_term.astype(jnp.bfloat16), "expert", scatter_dimension=1, tiled=True
        ).astype(jnp.float32),
        lax.psum_scatter(
            din_term.astype(jnp.bfloat16), "expert", scatter_dimension=1, tiled=True
        ).astype(jnp.float32),
    )
    return (
        out_total.astype(jnp.bfloat16),
        din_total.astype(jnp.bfloat16),
        grad_w_gate,
        grad_w_up,
        grad_w_down,
    )


def solution(mesh):
    return jax.shard_map(
        on_device,
        mesh=mesh,
        in_specs=(
            P(("dp", "sequence"), None),
            P(("dp", "sequence"), None),
            P(("dp", "sequence"), None),
            P(("dp", "sequence"), None),
            P("expert", ("dp", "sequence"), None),
            P("expert", ("dp", "sequence"), None),
            P("expert", ("dp", "sequence"), None),
        ),
        out_specs=(
            P(("dp", "sequence"), "expert"),
            P(("dp", "sequence"), "expert"),
            P("expert", ("dp", "sequence"), None),
            P("expert", ("dp", "sequence"), None),
            P("expert", ("dp", "sequence"), None),
        ),
        check_vma=False,
    )
```

profile of v0, /device:TPU:2, one launch (start us, length us, event | category | flops | bytes accessed | tf_op | source)
XLA Modules:
  0.0 552.4 jit_solution(13933945983895416042)
XLA Ops:
  10.0 1.7 fusion.11
  13.7 88.2 %all-gather.16.cloned.1.call-done = bf16[64,10,3072]{2,1,0:T(8,128)(2,1)} async-done(((bf16[1,10,3072]{2,1,0:T(8,128)(2,1)}), bf16[64,10,3072]{2,1,0:T(8,128)(2,1)}) %all-gather.16.cloned.1.call-update) | async-done | bytes 3932176 | tf_op jit(solution)/shard_map/all_gather | solution.py:36
  103.8 85.1 %all-gather.18.cloned.1.call-done = bf16[64,10,3072]{2,1,0:T(8,128)(2,1)} async-done(((bf16[1,10,3072]{2,1,0:T(8,128)(2,1)}), bf16[64,10,3072]{2,1,0:T(8,128)(2,1)}) %all-gather.18.cloned.1.call-update) | async-done | bytes 3932176 | tf_op jit(solution)/shard_map/all_gather | solution.py:37
  191.7 41.3 %all-gather.10.cloned.1.call-done = bf16[1,512,3072]{2,1,0:T(8,128)(2,1)} async-done(((bf16[1,128,3072]{2,1,0:T(8,128)(2,1)}), bf16[1,512,3072]{2,1,0:T(8,128)(2,1)}) %all-gather.10.cloned.1.call-update) | async-done | bytes 3145744 | tf_op jit(solution)/shard_map/all_gather | solution.py:48
  232.9 3.1 fusion.20
  236.0 43.9 %all-gather.12.cloned.1.call-done = bf16[1,512,3072]{2,1,0:T(8,128)(2,1)} async-done(((bf16[1,128,3072]{2,1,0:T(8,128)(2,1)}), bf16[1,512,3072]{2,1,0:T(8,128)(2,1)}) %all-gather.12.cloned.1.call-update) | async-done | bytes 3145744 | tf_op jit(solution)/shard_map/all_gather | solution.py:49
  280.0 3.1 fusion.16
  283.0 43.9 %all-gather.14.cloned.1.call-done = bf16[1,512,3072]{2,1,0:T(8,128)(2,1)} async-done(((bf16[1,128,3072]{2,1,0:T(8,128)(2,1)}), bf16[1,512,3072]{2,1,0:T(8,128)(2,1)}) %all-gather.14.cloned.1.call-update) | async-done | bytes 3145744 | tf_op jit(solution)/shard_map/all_gather | solution.py:50
  327.0 3.3 multiply_convert_fusion
  330.3 1.7 fusion.5
  334.0 1.7 fusion.4
  336.7 2.3 reduce.5
  340.1 4.6 all-to-all-start
  347.1 2.3 reduce.6
  350.5 4.8 all-to-all-start.1
  355.8 2.3 reduce.7
  360.1 4.8 all-to-all-start.2
  365.7 4.7 fusion.8
  370.4 88.1 %all-reduce.5.cloned.1.call-done = (bf16[1,160,3072]{2,1,0:T(8,128)(2,1)}, bf16[1,160,3072]{2,1,0:T(8,128)(2,1)}) async-done(((bf16[1,160,3072]{2,1,0:T(8,128)(2,1)}, bf16[1,160,3072]{2,1,0:T(8,128)(2,1)}), (bf16[1,160,3072]{2,1,0:T(8,128)(2,1)}, bf16[1,160,3072]{2,1,0:T(8,128)(2,1)})) %all-reduce.5.cloned.1.call-update) | async-done | bytes 1966096
  461.0 4.7 fusion.7
  468.9 4.7 fusion.6
  473.6 27.9 %reduce-scatter.9.cloned.1.call-done = bf16[384,24]{1,0:T(8,128)(2,1)} async-done(((bf16[3072,24]{1,0:T(8,128)(2,1)}), bf16[384,24]{1,0:T(8,128)(2,1)}) %reduce-scatter.9.cloned.1.call-update) | async-done | bytes 18448
  503.0 41.0 %reduce-scatter.11.cloned.1.call-done = bf16[384,24]{1,0:T(8,128)(2,1)} async-done(((bf16[3072,24]{1,0:T(8,128)(2,1)}), bf16[384,24]{1,0:T(8,128)(2,1)}) %reduce-scatter.11.cloned.1.call-update) | async-done | bytes 18448
  544.0 1.6 copy.59
  (66 shorter events, 26.6 us)
Async XLA Ops:
  7.2 1.1 copy-start
  7.2 94.7 %all-gather.16.cloned.1.call-start = ((), (), s32[]{:S(2)}) async-start(), calls=%async_computation.8 | async-start | bytes 6389760 | tf_op jit(solution)/shard_map/all_gather | solution.py:36
  9.1 179.9 %all-gather.18.cloned.1.call-start = ((), (), s32[]{:S(2)}) async-start(), calls=%async_computation.9 | async-start | bytes 6389760 | tf_op jit(solution)/shard_map/all_gather | solution.py:37
  11.7 221.2 %all-gather.10.cloned.1.call-start = ((), (), s32[]{:S(2)}) async-start(), calls=%async_computation.5 | async-start | bytes 3932160 | tf_op jit(solution)/shard_map/all_gather | solution.py:48
  12.4 267.5 %all-gather.12.cloned.1.call-start = ((), (), s32[]{:S(2)}) async-start(), calls=%async_computation.6 | async-start | bytes 3932160 | tf_op jit(solution)/shard_map/all_gather | solution.py:49
  13.0 314.0 %all-gather.14.cloned.1.call-start = ((), (), s32[]{:S(2)}) async-start(), calls=%async_computation.7 | async-start | bytes 3932160 | tf_op jit(solution)/shard_map/all_gather | solution.py:50
  13.6 444.9 %all-reduce.5.cloned.1.call-start = ((), (), s32[]{:S(2)}) async-start(), calls=%async_computation.12 | async-start | bytes 3932160
  236.0 91.0 %copy-start.4 = (bf16[160,3072]{1,0:T(8,128)(2,1)S(1)}, bf16[160,3072]{1,0:T(8,128)(2,1)}, u32[]{:S(2)}) copy-start(bf16[160,3072]{1,0:T(8,128)(2,1)} %reshape.384) | copy-start | bytes 2949124
  327.0 3.3 copy-start.3
  330.3 2.2 copy-start.1
  332.0 2.0 copy-start.2
  340.1 10.4 %all-to-all-start = ((bf16[4,2,10240]{2,1,0:T(2,128)(2,1)}), bf16[4,2,10240]{2,1,0:T(2,128)(2,1)S(1)}, u32[]{:S(2)}, u32[]{:S(2)}) async-start(bf16[4,2,10240]{2,1,0:T(2,128)(2,1)} %reshape.421), calls=%async_computation | async-start | bytes 327680 | tf_op jit(solution)/shard_map/all_to_all | solution.py:72
  350.5 9.6 %all-to-all-start.1 = ((bf16[4,2,10240]{2,1,0:T(2,128)(2,1)}), bf16[4,2,10240]{2,1,0:T(2,128)(2,1)S(1)}, u32[]{:S(2)}, u32[]{:S(2)}) async-start(bf16[4,2,10240]{2,1,0:T(2,128)(2,1)} %reshape.423), calls=%async_computation.1 | async-start | bytes 327680 | tf_op jit(solution)/shard_map/all_to_all | solution.py:73
  360.1 105.6 %all-to-all-start.2 = ((bf16[4,2,10240]{2,1,0:T(2,128)(2,1)}), bf16[4,2,10240]{2,1,0:T(2,128)(2,1)S(1)}, u32[]{:S(2)}, u32[]{:S(2)}) async-start(bf16[4,2,10240]{2,1,0:T(2,128)(2,1)} %reshape.425), calls=%async_computation.2 | async-start | bytes 327680 | tf_op jit(solution)/shard_map/all_to_all | solution.py:74
  364.9 136.6 %reduce-scatter.9.cloned.1.call-start = ((), (), s32[]{:S(2)}) async-start(), calls=%async_computation.10 | async-start | bytes 884736
  461.0 83.1 %reduce-scatter.11.cloned.1.call-start = ((), (), s32[]{:S(2)}) async-start(), calls=%async_computation.11 | async-start | bytes 884736
Sparse Core Ops, SparseCore 0:
  11.9 89.9 all-gather.15
  105.8 83.1 all-gather.17
  191.0 41.8 all-gather.9
  234.9 45.0 all-gather.11
  281.9 45.0 all-gather.13
  335.8 122.6 all-reduce.4
  461.3 40.0 reduce-scatter.8
  504.3 39.6 reduce-scatter.10
where the time goes:
time: 553 us; the launch traced here: 552 us
  waiting for transfers between devices  461 us (83%)
  matrix products  32.6 us (6%)
  local copies, waits for them, and re-layouts  20.4 us (4%)
  between operations  15 us (3%)
  starting transfers between devices  14.5 us (3%)
  other arithmetic  8.64 us (2%)
    unnamed x11, waiting for transfers between devices  159 us
    all_gather x1, waiting for transfers between devices, on_device(): lax.all_gather(slot_tokens, ('dp', 'sequence'), axis=1, tiled=True)  88.2 us
    all_gather x1, waiting for transfers between devices, on_device(): lax.all_gather(scaled_grad, ('dp', 'sequence'), axis=1, tiled=True)  85.1 us
    all_gather x1, waiting for transfers between devices, on_device(): lax.all_gather(w_down, 'sequence', axis=1, tiled=True)  43.9 us
    all_gather x1, waiting for transfers between devices, on_device(): lax.all_gather(w_up, 'sequence', axis=1, tiled=True)  43.9 us
    all_gather x1, waiting for transfers between devices, on_device(): lax.all_gather(w_gate, 'sequence', axis=1, tiled=True)  41.3 us
    unnamed x24, local copies, waits for them, and re-layouts  16.3 us
  transfers between devices with their start and end apart: 11, of which 8 were waited for; matrix products, arithmetic and copies ran while one was open for 9% of the time, Pallas kernels for 0%

commit v1 on v0

--- a/solution.py
+++ b/solution.py
@@ -46,7 +46,9 @@
     )
     gate_rows, up_rows, down_rows = (
         lax.all_gather(w_gate, "sequence", axis=1, tiled=True),
-        lax.all_gather(w_up, "sequence", axis=1, tiled=True),
+        jnp.concatenate(
+            lax.all_to_all(jnp.stack([w_up] * lax.axis_size("sequence")), "sequence", 0, 0), axis=1
+        ),
         lax.all_gather(w_down, "sequence", axis=1, tiled=True),
     )
     pre_gate = jnp.einsum("erd,ehd->erh", own_tok, gate_rows, preferred_element_type=jnp.float32)

time: 553 us -> 518 us (0.937)
  waiting for transfers between devices: 461 us -> 405 us
  starting transfers between devices: 14.5 us -> 24 us
  local copies, waits for them, and re-layouts: 20.4 us -> 29.4 us
    all_gather x1 -> x0, waiting for transfers between devices: 43.9 us -> none  [on_device(): lax.all_gather(w_up, 'sequence', axis=1, tiled=True)]
    all_to_all x0 -> x1, starting transfers between devices: none -> 9.55 us  [on_device(): lax.all_to_all(jnp.stack([w_up] * lax.axis_size('sequence')), 'sequence',...]
    another operation x3 -> x4, local copies, waits for them, and re-layouts: 1.66 us -> 7.95 us
    all_gather x1, waiting for transfers between devices: 41.3 us -> 35.7 us  [on_device(): lax.all_gather(w_gate, 'sequence', axis=1, tiled=True)]
    unnamed x24 -> x26, local copies, waits for them, and re-layouts: 16.3 us -> 18.2 us
    unnamed x11 -> x10, waiting for transfers between devices: 159 us -> 157 us
  transfers between devices with their start and end apart: 11 -> 11, of which waited for: 8 -> 7; matrix products, arithmetic and copies ran while one was open for 9% -> 12% of each run, Pallas kernels for 0% -> 0%
where the time goes in v1:
time: 518 us; the launch traced here: 516 us
  waiting for transfers between devices  405 us (78%)
  matrix products  34.1 us (7%)
  local copies, waits for them, and re-layouts  29.4 us (6%)
  starting transfers between devices  24 us (5%)
  between operations  15 us (3%)
  other arithmetic  8.64 us (2%)
    unnamed x10, waiting for transfers between devices  157 us
    all_gather x1, waiting for transfers between devices, on_device(): lax.all_gather(slot_tokens, ('dp', 'sequence'), axis=1, tiled=True)  87.5 us
    all_gather x1, waiting for transfers between devices, on_device(): lax.all_gather(scaled_grad, ('dp', 'sequence'), axis=1, tiled=True)  82 us
    all_gather x1, waiting for transfers between devices, on_device(): lax.all_gather(w_down, 'sequence', axis=1, tiled=True)  42.9 us
    all_gather x1, waiting for transfers between devices, on_device(): lax.all_gather(w_gate, 'sequence', axis=1, tiled=True)  35.7 us
    unnamed x26, local copies, waits for them, and re-layouts  18.2 us
  transfers between devices with their start and end apart: 11, of which 7 were waited for; matrix products, arithmetic and copies ran while one was open for 12% of the time, Pallas kernels for 0%

profile of v1, /device:TPU:2, one launch (start us, length us, event | category | flops | bytes accessed | tf_op | source)
XLA Modules:
  0.0 516.4 jit_solution(13842493015867050518)
XLA Ops:
  13.0 3.2 stack.2
  16.2 9.5 %all-to-all-start = ((bf16[4,1,128,3072]{3,2,1,0:T(8,128)(2,1)}), bf16[4,1,128,3072]{3,2,1,0:T(8,128)(2,1)S(1)}, u32[]{:S(2)}, u32[]{:S(2)}) async-start(bf16[4,1,128,3072]{3,2,1,0:T(8,128)(2,1)} %stack.2), calls=%async_computation | async-start | bytes 6291456 | tf_op jit(solution)/shard_map/all_to_all | solution.py:50
  25.7 87.5 %all-gather.13.cloned.1.call-done = bf16[64,10,3072]{2,1,0:T(8,128)(2,1)} async-done(((bf16[1,10,3072]{2,1,0:T(8,128)(2,1)}), bf16[64,10,3072]{2,1,0:T(8,128)(2,1)}) %all-gather.13.cloned.1.call-update) | async-done | bytes 3932176 | tf_op jit(solution)/shard_map/all_gather | solution.py:36
  113.2 2.8 dynamic-slice_bitcast_fusion.1
  118.3 82.0 %all-gather.15.cloned.1.call-done = bf16[64,10,3072]{2,1,0:T(8,128)(2,1)} async-done(((bf16[1,10,3072]{2,1,0:T(8,128)(2,1)}), bf16[64,10,3072]{2,1,0:T(8,128)(2,1)}) %all-gather.15.cloned.1.call-update) | async-done | bytes 3932176 | tf_op jit(solution)/shard_map/all_gather | solution.py:37
  200.3 2.8 dynamic-slice_bitcast_fusion
  203.0 2.4 reshape.390
  205.4 3.1 fusion.40
  208.6 35.7 %all-gather.9.cloned.1.call-done = bf16[1,512,3072]{2,1,0:T(8,128)(2,1)} async-done(((bf16[1,128,3072]{2,1,0:T(8,128)(2,1)}), bf16[1,512,3072]{2,1,0:T(8,128)(2,1)}) %all-gather.9.cloned.1.call-update) | async-done | bytes 3145744 | tf_op jit(solution)/shard_map/all_gather | solution.py:48
  244.3 4.1 fusion.17
  248.4 42.9 %all-gather.11.cloned.1.call-done = bf16[1,512,3072]{2,1,0:T(8,128)(2,1)} async-done(((bf16[1,128,3072]{2,1,0:T(8,128)(2,1)}), bf16[1,512,3072]{2,1,0:T(8,128)(2,1)}) %all-gather.11.cloned.1.call-update) | async-done | bytes 3145744 | tf_op jit(solution)/shard_map/all_gather | solution.py:52
  291.3 3.7 multiply_convert_fusion
  301.7 2.3 reduce.5
  305.1 4.6 all-to-all-start.1
  312.1 2.3 reduce.6
  315.6 4.8 all-to-all-start.2
  320.9 2.3 reduce.7
  325.1 4.8 all-to-all-start.3
  330.8 4.7 fusion.8
  335.5 87.1 %all-reduce.5.cloned.1.call-done = (bf16[1,160,3072]{2,1,0:T(8,128)(2,1)}, bf16[1,160,3072]{2,1,0:T(8,128)(2,1)}) async-done(((bf16[1,160,3072]{2,1,0:T(8,128)(2,1)}, bf16[1,160,3072]{2,1,0:T(8,128)(2,1)}), (bf16[1,160,3072]{2,1,0:T(8,128)(2,1)}, bf16[1,160,3072]{2,1,0:T(8,128)(2,1)})) %all-reduce.5.cloned.1.call-update) | async-done | bytes 1966096
  425.2 4.7 fusion.7
  433.1 4.7 fusion.6
  437.7 27.7 %reduce-scatter.9.cloned.1.call-done = bf16[384,24]{1,0:T(8,128)(2,1)} async-done(((bf16[3072,24]{1,0:T(8,128)(2,1)}), bf16[384,24]{1,0:T(8,128)(2,1)}) %reduce-scatter.9.cloned.1.call-update) | async-done | bytes 18448
  467.1 41.0 %reduce-scatter.11.cloned.1.call-done = bf16[384,24]{1,0:T(8,128)(2,1)} async-done(((bf16[3072,24]{1,0:T(8,128)(2,1)}), bf16[384,24]{1,0:T(8,128)(2,1)}) %reduce-scatter.11.cloned.1.call-update) | async-done | bytes 18448
  (68 shorter events, 30.6 us)
Async XLA Ops:
  7.2 1.1 copy-start
  7.2 106.0 %all-gather.13.cloned.1.call-start = ((), (), s32[]{:S(2)}) async-start(), calls=%async_computation.8 | async-start | bytes 6389760 | tf_op jit(solution)/shard_map/all_gather | solution.py:36
  9.1 191.2 %all-gather.15.cloned.1.call-start = ((), (), s32[]{:S(2)}) async-start(), calls=%async_computation.9 | async-start | bytes 6389760 | tf_op jit(solution)/shard_map/all_gather | solution.py:37
  11.7 232.6 %all-gather.9.cloned.1.call-start = ((), (), s32[]{:S(2)}) async-start(), calls=%async_computation.6 | async-start | bytes 3932160 | tf_op jit(solution)/shard_map/all_gather | solution.py:48
  12.4 278.9 %all-gather.11.cloned.1.call-start = ((), (), s32[]{:S(2)}) async-start(), calls=%async_computation.7 | async-start | bytes 3932160 | tf_op jit(solution)/shard_map/all_gather | solution.py:52
  16.2 189.2 %all-to-all-start = ((bf16[4,1,128,3072]{3,2,1,0:T(8,128)(2,1)}), bf16[4,1,128,3072]{3,2,1,0:T(8,128)(2,1)S(1)}, u32[]{:S(2)}, u32[]{:S(2)}) async-start(bf16[4,1,128,3072]{3,2,1,0:T(8,128)(2,1)} %stack.2), calls=%async_computation | async-start | bytes 6291456 | tf_op jit(solution)/shard_map/all_to_all | solution.py:50
  25.7 396.9 %all-reduce.5.cloned.1.call-start = ((), (), s32[]{:S(2)}) async-start(), calls=%async_computation.12 | async-start | bytes 3932160
  291.3 3.8 copy-start.2
  295.0 3.1 copy-start.5
  295.1 3.1 copy-start.3
  295.1 2.4 copy-start.1
  299.9 11.8 %copy-start.4 = (bf16[160,512]{1,0:T(8,128)(2,1)S(1)}, bf16[160,512]{1,0:T(8,128)(2,1)}, u32[]{:S(2)}) copy-start(bf16[160,512]{1,0:T(8,128)(2,1)} %copy-done.3) | copy-start | bytes 491524
  305.1 10.4 %all-to-all-start.1 = ((bf16[4,2,10240]{2,1,0:T(2,128)(2,1)}), bf16[4,2,10240]{2,1,0:T(2,128)(2,1)S(1)}, u32[]{:S(2)}, u32[]{:S(2)}) async-start(bf16[4,2,10240]{2,1,0:T(2,128)(2,1)} %reshape.427), calls=%async_computation.1 | async-start | bytes 327680 | tf_op jit(solution)/shard_map/all_to_all | solution.py:74
  315.6 9.6 %all-to-all-start.2 = ((bf16[4,2,10240]{2,1,0:T(2,128)(2,1)}), bf16[4,2,10240]{2,1,0:T(2,128)(2,1)S(1)}, u32[]{:S(2)}, u32[]{:S(2)}) async-start(bf16[4,2,10240]{2,1,0:T(2,128)(2,1)} %reshape.429), calls=%async_computation.2 | async-start | bytes 327680 | tf_op jit(solution)/shard_map/all_to_all | solution.py:75
  325.1 104.7 %all-to-all-start.3 = ((bf16[4,2,10240]{2,1,0:T(2,128)(2,1)}), bf16[4,2,10240]{2,1,0:T(2,128)(2,1)S(1)}, u32[]{:S(2)}, u32[]{:S(2)}) async-start(bf16[4,2,10240]{2,1,0:T(2,128)(2,1)} %reshape.431), calls=%async_computation.3 | async-start | bytes 327680 | tf_op jit(solution)/shard_map/all_to_all | solution.py:76
  330.0 135.5 %reduce-scatter.9.cloned.1.call-start = ((), (), s32[]{:S(2)}) async-start(), calls=%async_computation.10 | async-start | bytes 884736
  425.1 82.9 %reduce-scatter.11.cloned.1.call-start = ((), (), s32[]{:S(2)}) async-start(), calls=%async_computation.11 | async-start | bytes 884736
Sparse Core Ops, SparseCore 0:
  11.9 101.2 all-gather.12
  117.1 83.1 all-gather.14
  202.4 41.8 all-gather.8
  246.2 45.0 all-gather.10
  300.0 122.6 all-reduce.4
  425.3 40.0 reduce-scatter.8
  468.3 39.6 reduce-scatter.10
